TPU v7x, 32 devices: a whole 2x2x4 slice. The times are simulated.
32 devices in a mesh: rep: 2 (over x), seq: 8 (over z, y), tp: 2 (over core).
Axes of the slice: x: 2, y: 2, z: 4, core: 2. Of those that a mesh axis runs over, the one named last changes fastest.
Arguments:
- prefill_query: bfloat16 [8192, 2048], P(('rep', 'seq'), 'tp'), parts along dimension 0, may hold values from -50 to 50
- prefill_key: bfloat16 [8192, 512], P(('rep', 'seq'), 'tp'), parts along dimension 0, may hold values from -6 to 6
- prefill_value: bfloat16 [8192, 512], P(('rep', 'seq'), 'tp'), parts along dimension 0, may hold values from -6 to 6
- doc_ids: int32 [8192], P('rep'), parts along dimension 0, may hold values from 0 to 3, never falling along the last dimension, each value on 1 to 2048 neighbouring positions
- head_window: int32 [16], P('tp'), may hold values from 1024 to 4096, as said below
- dec_query: bfloat16 [128, 2048], P('rep', 'tp'), parts along dimension 0, may hold values from -50 to 50
- dec_key: bfloat16 [128, 512], P('rep', 'tp'), parts along dimension 0, may hold values from -6 to 6
- dec_value: bfloat16 [128, 512], P('rep', 'tp'), parts along dimension 0, may hold values from -6 to 6
- cache_key: bfloat16 [65536, 512], P(('rep', 'seq'), 'tp'), parts along dimension 0, may hold values from -6 to 6
- cache_value: bfloat16 [65536, 512], P(('rep', 'seq'), 'tp'), parts along dimension 0, may hold values from -6 to 6
- page_order: int32 [512], P(('rep', 'seq')), parts along dimension 0, may hold values from 0 to 255, each once
- lengths: int32 [128], P('rep'), parts along dimension 0, may hold values from 1 to 512, 16384 in all
- out_proj: bfloat16 [2048, 4096], P('tp'), may hold values from -0.125 to 0.125
Outputs:
- prompt_out: bfloat16 [8192, 4096], P(('rep', 'seq', 'tp')), parts along dimension 0
- decode_out: bfloat16 [128, 4096], P(('rep', 'tp')), parts along dimension 0
There are 2 independent parts, one for each index of `rep`. A program takes and returns all parts, laid end to end along the dimension named above; an argument that names none is the same for every part. Nothing has to cross between parts.
Inputs may be any that keep to these rules, and one draw needn't show every extreme that they name: `head_window`: some head has window 4096.
All inputs are finite; a program needn't handle non-finite values.
Results may differ from a plain program's by a relative error of at most 0.015.
Values may be sent and summed in bfloat16 or wider, within the bound.
A program may use at most 256 MiB of HBM per device.

v0:
```python
from functools import partial
import math

import jax
import jax.numpy as jnp
from jax import lax
from jax.sharding import PartitionSpec as P

HD = 128
WINDOW = 4096
PAGE = 128


masked_score = -1e30


def combined_all(array, axis, combine):
    everything = jax.tree.map(
        lambda part, kind: lax.all_gather(part.astype(kind), axis),
        array,
        (jnp.bfloat16, jnp.bfloat16, jnp.bfloat16),
    )

    def take(k):
        return jax.tree.map(lambda part, own: part[k].astype(own.dtype), everything, array)

    return lax.fori_loop(
        1, lax.axis_size(axis), lambda k, so_far: combine(so_far, take(k)), take(0)
    )


def round_half(values):
    return lax.optimization_barrier(values.astype(jnp.bfloat16)).astype(jnp.float32)


def attend_block(
    carry, piece, start, queries, query_pos, query_doc, doc_ids, windows, scale_factor
):
    key_piece, value_piece = piece
    count_rows = key_piece.shape[0]
    kv_local = windows.shape[0]
    head_dim = key_piece.shape[1] // kv_local
    key_pos = start + jnp.arange(count_rows, dtype=jnp.int32)
    key_doc = lax.dynamic_slice_in_dim(doc_ids, jnp.maximum(start, 0), count_rows, 0)
    gap = query_pos[:, None] - key_pos[None, :]
    allowed = (key_pos[None, :] >= 0) & (gap >= 0) & (query_doc[:, None] == key_doc[None, :])
    allowed = allowed[None, None] & (gap[None, None] < windows[:, :, None, None])
    scores = (
        jnp.einsum(
            "tkgd,skd->kgts",
            queries,
            key_piece.reshape(count_rows, kv_local, head_dim),
            preferred_element_type=jnp.float32,
        )
        * scale_factor
    )
    scores = jnp.where(allowed, scores, masked_score)
    running, totals, accum = carry
    fresh = jnp.maximum(running, jnp.max(scores, axis=-1))
    weights = jnp.where(allowed, jnp.exp(scores - fresh[..., None]), 0.0)
    totals = jnp.sum(weights, axis=-1)
    accum = jnp.einsum(
        "kgts,skd->kgtd",
        weights.astype(jnp.bfloat16),
        value_piece.reshape(count_rows, kv_local, head_dim),
        preferred_element_type=jnp.float32,
    )
    return (fresh, totals, accum)


def window_fold(carry, piece, start, update, my_start, tok_rows):
    piece_rows = piece[0].shape[0]
    needed = min(piece_rows, WINDOW + tok_rows)
    if needed < piece_rows:
        offset = jnp.clip(my_start - WINDOW - start, 0, piece_rows - needed).astype(jnp.int32)
        piece = (
            lax.dynamic_slice_in_dim(piece[0], offset, needed, 0),
            lax.dynamic_slice_in_dim(piece[1], offset, needed, 0),
        )
        start = start + offset
    return update(carry, piece, start)


def combine_parts(first, second):
    top = jnp.maximum(first[0], second[0])
    left = jnp.exp(first[0] - top)
    right = jnp.exp(second[0] - top)
    return (
        top,
        first[1] * left + second[1] * right,
        first[2] * left[..., None] + second[2] * right[..., None],
    )


def project_rows(rows_matrix, out_proj):
    return jnp.dot(rows_matrix, out_proj, preferred_element_type=jnp.float32)


def on_device(
    prefill_query,
    prefill_key,
    prefill_value,
    doc_ids,
    head_window,
    dec_query,
    dec_key,
    dec_value,
    cache_key,
    cache_value,
    page_order,
    lengths,
    out_proj,
):
    tok_rows = prefill_query.shape[0]
    kv_local = prefill_key.shape[1] // HD
    heads_local = prefill_query.shape[1] // HD
    group_size = heads_local // kv_local
    scale_factor = 1.0 / math.sqrt(HD)
    seq_index = lax.axis_index("seq")
    my_start = seq_index * tok_rows
    queries = prefill_query.reshape(tok_rows, kv_local, group_size, HD)
    query_pos = my_start + jnp.arange(tok_rows, dtype=jnp.int32)
    query_doc = lax.dynamic_slice_in_dim(doc_ids, my_start, tok_rows, 0)
    windows = head_window.reshape(kv_local, group_size)
    update = partial(
        attend_block,
        queries=queries,
        query_pos=query_pos,
        query_doc=query_doc,
        doc_ids=doc_ids,
        windows=windows,
        scale_factor=scale_factor,
    )
    initial = (
        jnp.full((kv_local, group_size, tok_rows), masked_score, jnp.float32),
        jnp.zeros((kv_local, group_size, tok_rows), jnp.float32),
        jnp.zeros((kv_local, group_size, tok_rows, HD), jnp.float32),
    )
    windowed = partial(window_fold, update=update, my_start=my_start, tok_rows=tok_rows)
    carry = windowed(
        initial,
        (
            lax.all_gather(prefill_key, "seq", axis=0, tiled=True),
            lax.all_gather(prefill_value, "seq", axis=0, tiled=True),
        ),
        jnp.int32(0),
    )
    running, totals, accum = carry
    prompt_attn = (
        (accum / totals[..., None])
        .transpose(2, 0, 1, 3)
        .reshape(tok_rows, heads_local * HD)
        .astype(jnp.bfloat16)
    )
    page_count = page_order.shape[0]
    request_count = dec_query.shape[0]
    pages_request = page_count * lax.axis_size("seq") // request_count
    owner = page_order // pages_request
    slot_index = page_order % pages_request
    page_queries = dec_query[owner].reshape(page_count, kv_local, group_size, HD)
    page_keys = cache_key.reshape(page_count, PAGE, kv_local, HD)
    page_values = cache_value.reshape(page_count, PAGE, kv_local, HD)
    scores = (
        jnp.einsum("pkgd,ptkd->pkgt", page_queries, page_keys, preferred_element_type=jnp.float32)
        * scale_factor
    )
    positions = slot_index[:, None] * PAGE + jnp.arange(PAGE, dtype=jnp.int32)[None, :]
    valid = (positions < lengths[owner][:, None])[:, None, None, :]
    scores = jnp.where(valid, scores, masked_score)
    page_top = jnp.max(scores, axis=-1)
    weights = jnp.where(valid, jnp.exp(scores - page_top[..., None]), 0.0)
    page_total = jnp.sum(weights, axis=-1)
    page_accum = jnp.einsum(
        "pkgt,ptkd->pkgd",
        weights.astype(jnp.bfloat16),
        page_values,
        preferred_element_type=jnp.float32,
    )
    member = owner[None, :] == jnp.arange(request_count, dtype=jnp.int32)[:, None]
    request_top = jnp.max(jnp.where(member[:, :, None, None], page_top[None], masked_score), axis=1)
    rescale = jnp.exp(page_top - request_top[owner])
    member_float = member.astype(jnp.float32)
    request_total = jnp.dot(
        member_float,
        (page_total * rescale).reshape(page_count, -1),
        precision=lax.Precision.HIGHEST,
    ).reshape(request_count, kv_local, group_size)
    request_accum = jnp.dot(
        member_float,
        (page_accum * rescale[..., None]).reshape(page_count, -1),
        precision=lax.Precision.HIGHEST,
    ).reshape(request_count, kv_local, group_size, HD)
    merged = combined_all((request_top, request_total, request_accum), "seq", combine_parts)
    merged_top, merged_total, merged_accum = merged
    dec_queries = dec_query.reshape(request_count, kv_local, group_size, HD)
    own_scores = (
        jnp.einsum(
            "rkgd,rkd->rkg",
            dec_queries,
            dec_key.reshape(request_count, kv_local, HD),
            preferred_element_type=jnp.float32,
        )
        * scale_factor
    )
    final_top = jnp.maximum(merged_top, own_scores)
    shrink = jnp.exp(merged_top - final_top)
    own_weights = jnp.exp(own_scores - final_top)
    final_total = merged_total * shrink + own_weights
    own_values = dec_value.reshape(request_count, kv_local, 1, HD).astype(jnp.float32)
    final_accum = merged_accum * shrink[..., None] + round_half(own_weights)[..., None] * own_values
    decode_attn = (
        (final_accum / final_total[..., None])
        .reshape(request_count, heads_local * HD)
        .astype(jnp.bfloat16)
    )
    prompt_out = lax.psum_scatter(
        project_rows(prompt_attn, out_proj).astype(jnp.bfloat16),
        "tp",
        scatter_dimension=0,
        tiled=True,
    )
    decode_out = lax.psum_scatter(
        project_rows(decode_attn, out_proj).astype(jnp.bfloat16),
        "tp",
        scatter_dimension=0,
        tiled=True,
    )
    return (prompt_out, decode_out)


def solution(mesh):
    placed = (
        P(("rep", "seq"), "tp"),
        P(("rep", "seq"), "tp"),
        P(("rep", "seq"), "tp"),
        P("rep"),
        P("tp"),
        P("rep", "tp"),
        P("rep", "tp"),
        P("rep", "tp"),
        P(("rep", "seq"), "tp"),
        P(("rep", "seq"), "tp"),
        P(("rep", "seq")),
        P("rep"),
        P("tp", None),
    )
    return jax.shard_map(
        on_device,
        mesh=mesh,
        in_specs=placed,
        out_specs=(P(("rep", "seq", "tp"), None), P(("rep", "tp"), None)),
        check_vma=False,
    )
```

profile of v0, /device:TPU:18, one launch (start us, length us, event | category | flops | bytes accessed | tf_op | source)
XLA Modules:
  0.0 255.3 jit_solution(7841837470292784947)
XLA Ops:
  7.2 0.8 compare_select_fusion
  8.1 0.7 gather_fusion
  8.8 1.6 gather_fusion.1
  10.4 4.0 %reshape.218 = bf16[32,128,2,128]{3,2,1,0:T(2,128)(2,1)} reshape(bf16[4096,256]{1,0:T(8,128)(2,1)} %param.23) | data formatting | bytes 4194304 | tf_op jit(solution)/shard_map/reshape | solution.py:161
  14.5 2.9 %fusion.48 = (f32[32,2,4]{2,1,0:T(2,128)S(1)}, f32[32,2,4,128]{3,2,1,0:T(4,128)S(1)}) fusion(bf16[32,2,4,128]{3,2,1,0:T(4,128)(2,1)S(1)} %reshape.217, bf16[32,128,2,128]{3,2,1,0:T(2,128)(2,1)} %reshape.218, pred[32,128]{1,0:T(8,128)(4,1)S(1)} %add_compare_fusion), kind=kOutput, calls=%fused_computation.80 | convolution fusion | flops 8486656 | bytes 2298880 | tf_op jit(solution)/shard_map/pkgd,ptkd->pkgt/dot_general | solution.py:164
  18.8 2.0 reshape.219
  20.8 2.3 fusion.20
  23.3 1.0 convolution_convert_fusion.2
  24.4 0.8 copy.99
  25.3 0.7 all-gather.9.cloned.1.call-update
  26.6 26.7 %all-gather.1 = bf16[512,2,4]{2,1,0:T(2,128)(2,1)S(1)} all-gather(bf16[64,2,4]{2,1,0:T(2,128)(2,1)S(1)} %copy.109), channel_id=3, replica_groups=mesh['rep'=2,'seq'=8,'tp'=2] {'seq'}, dimensions={0}, use_global_device_ids=true | all-gather | bytes 9216 | tf_op jit(solution)/shard_map/all_gather | solution.py:19
  53.4 0.8 copy.117
  54.3 31.5 %all-gather = bf16[512,2,4]{2,1,0:T(2,128)(2,1)S(1)} all-gather(bf16[64,2,4]{2,1,0:T(2,128)(2,1)S(1)} %copy.106), channel_id=2, replica_groups=mesh['rep'=2,'seq'=8,'tp'=2] {'seq'}, dimensions={0}, use_global_device_ids=true | all-gather | bytes 9216 | tf_op jit(solution)/shard_map/all_gather | solution.py:19
  85.9 0.8 copy.116
  87.0 0.7 copy.127
  87.7 0.7 reshape.229
  88.3 4.4 %iota_subtract_fusion = s32[512,4096]{0,1:T(8,128)} fusion(s32[512]{0:T(512)S(1)} %iota_add_fusion), kind=kLoop, calls=%fused_computation.20 | loop fusion | flops 2097152 | bytes 8390656 | tf_op jit(solution)/shard_map/sub | solution.py:45
  92.8 2.5 compare_and_fusion.1
  95.3 0.7 lt.62
  95.9 1.8 reshape.215
  97.8 0.9 slice_convert_fusion
  98.9 17.3 %while.19 = (s32[]{:T(128)}, f32[64,2,4]{0,2,1:T(4,128)S(1)}, f32[64,2,4]{0,2,1:T(4,128)S(1)}, f32[64,2,4,128]{3,2,1,0:T(4,128)S(1)}, bf16[8,64,2,4]{1,3,2,0:T(4...) while((s32[]{:T(128)}, f32[64,2,4]{0,2,1:T(4,128)S(1)}, ...), condition=%wide.region_7.8_spmd, body=%wide.region_6.7_spmd.sunk | while | flops 266245 | bytes 944279 | solution.py:27
  98.9 0.7 fusion.61
  99.9 0.9 constant_dynamic-slice_fusion.2
  101.4 0.7 fusion.61
  102.3 0.9 constant_dynamic-slice_fusion.2
  103.8 0.7 fusion.61
  104.8 0.9 constant_dynamic-slice_fusion.2
  106.3 0.7 fusion.61
  107.3 0.9 constant_dynamic-slice_fusion.2
  108.8 0.7 fusion.61
  109.8 0.9 constant_dynamic-slice_fusion.2
  111.3 0.7 fusion.61
  112.2 0.9 constant_dynamic-slice_fusion.2
  113.7 0.7 fusion.61
  114.7 0.9 constant_dynamic-slice_fusion.2
  116.2 0.7 fusion.37
  116.9 0.7 copy.119
  117.6 0.7 copy.120
  118.4 0.7 copy.121
  119.1 1.4 fusion.25
  120.6 5.8 %convolution_convert_fusion.1 = bf16[64,4096]{1,0:T(8,128)(2,1)} fusion(bf16[64,1024]{1,0:T(8,128)(2,1)S(1)} %convert_element_type.138, bf16[1024,4096]{1,0:T(8,128)(2,1)} %param.27), kind=kOutput, calls=%fused_computation.23 | convolution fusion | flops 537133056 | bytes 9043968 | tf_op jit(solution)/shard_map/dot_general | solution.py:96
  126.7 31.4 %fusion.3 = (f32[2,4,512]{2,1,0:T(4,128)S(1)}, f32[2,4096,512,4]{2,1,3,0:T(8,128)}) fusion(s32[2,4]{1,0:T(2,128)S(1)} %copy-done.4, s32[512,4096]{0,1:T(8,128)} %iota_subtract_fusion, pred[512,4096]{0,1:T(8,128)(4,1)S(1)} %compare_and_fusion.1, bf16[4096,2,128,1]{0,2,3,1:T(8,128)(2,1)} %bitcast.94, bf16[512,2,4,128]{3,2,1,0:T(4,128)(2,1)S(1)} %reshape.215), kind=kOutput, calls=%fused_computation.16 | convolution fusion | flops 4378849280 | bytes 80756768 | tf_op jit(solution)/shard_map/tkgd,skd->kgts/dot_general | solution.py:49
  158.1 28.4 %fusion.6 = f32[2,4,512]{2,1,0:T(4,128)S(1)} fusion(f32[2,4,512]{2,1,0:T(4,128)S(1)} %broadcast_maximum_fusion, f32[2,4096,512,4]{2,1,3,0:T(8,128)} %get-tuple-element.245, s32[2,4]{1,0:T(2,128)S(1)} %copy-done.4, s32[512,4096]{0,1:T(8,128)} %iota_subtract_fusion, pred[512,4096]{0,1:T(8,128)(4,1)S(1)} %compare_and_fusion.1), kind=kLoop, calls=%fused_computation.19 | loop fusion | flops 117436416 | bytes 77627424 | tf_op jit(solution)/shard_map/reduce_sum | solution.py:61
  186.5 4.1 %copy.102 = bf16[4096,256]{0,1:T(8,128)(2,1)} copy(bf16[4096,256]{1,0:T(8,128)(2,1)} %all-gather.9.cloned.1.call-done) | data formatting | bytes 4194304 | tf_op jit(solution)/shard_map/all_gather | solution.py:144
  190.5 31.1 %fusion.7 = bf16[512,2,4,128]{0,3,2,1:T(8,128)(2,1)S(1)} fusion(bf16[4096,2,128,1]{0,2,3,1:T(8,128)(2,1)} %bitcast.95, f32[2,4,512]{2,1,0:T(4,128)S(1)} %broadcast_maximum_fusion, f32[2,4096,512,4]{2,1,3,0:T(8,128)} %get-tuple-element.245, s32[2,4]{1,0:T(2,128)S(1)} %copy-done.4, s32[512,4096]{0,1:T(8,128)} %iota_subtract_fusion, ...), kind=kOutput, calls=%fused_computation.25 | convolution fusion | flops 4413456384 | bytes 80773152 | tf_op jit(solution)/shard_map/kgts,skd->kgtd/dot_general | solution.py:62
  221.7 9.5 %convolution_convert_fusion = bf16[512,4096]{1,0:T(8,128)(2,1)} fusion(bf16[512,1024]{0,1:T(8,128)(2,1)S(1)} %bitcast.106, bf16[1024,4096]{1,0:T(8,128)(2,1)} %param.27), kind=kOutput, calls=%fused_computation.22 | convolution fusion | flops 4297064448 | bytes 13631488 | tf_op jit(solution)/shard_map/dot_general | solution.py:96
  231.2 17.6 %reduce-scatter.3.cloned.1.call-done = bf16[256,4096]{1,0:T(8,128)(2,1)} async-done(((bf16[512,4096]{1,0:T(8,128)(2,1)}), bf16[256,4096]{1,0:T(8,128)(2,1)}) %reduce-scatter.3.cloned.1.call-update) | async-done | bytes 2097168 | tf_op jit(solution)/shard_map/reduce_scatter | solution.py:216
  (81 shorter events, 9.2 us)
Async XLA Ops:
  7.2 0.9 copy-start
  7.2 11.6 %copy-start.2 = (bf16[4096,256]{1,0:T(8,128)(2,1)S(1)}, bf16[4096,256]{1,0:T(8,128)(2,1)}, u32[]{:S(2)}) copy-start(bf16[4096,256]{1,0:T(8,128)(2,1)} %param.24) | copy-start | bytes 6291460
  7.2 90.6 %all-gather.11.cloned.1.call-start = ((), (), s32[]{:S(2)}) async-start(), calls=%async_computation.6 | async-start | bytes 1179648 | tf_op jit(solution)/shard_map/all_gather | solution.py:19
  10.4 14.0 %copy-start.3 = (bf16[512,256]{1,0:T(8,128)(2,1)S(1)}, bf16[512,256]{1,0:T(8,128)(2,1)}, u32[]{:S(2)}) copy-start(bf16[512,256]{1,0:T(8,128)(2,1)} %param.16) | copy-start | bytes 786436
  10.4 15.6 %copy-start.1 = (bf16[64,1024]{1,0:T(8,128)(2,1)S(1)}, bf16[64,1024]{1,0:T(8,128)(2,1)}, u32[]{:S(2)}) copy-start(bf16[64,1024]{1,0:T(8,128)(2,1)} %param.20) | copy-start | bytes 393220
  14.5 72.2 %copy-start.5 = (bf16[64,256]{1,0:T(8,128)(2,1)S(1)}, bf16[64,256]{1,0:T(8,128)(2,1)}, u32[]{:S(2)}) copy-start(bf16[64,256]{1,0:T(8,128)(2,1)} %param.21) | copy-start | bytes 98308
  14.5 73.2 %copy-start.6 = (bf16[64,256]{1,0:T(8,128)(2,1)S(1)}, bf16[64,256]{1,0:T(8,128)(2,1)}, u32[]{:S(2)}) copy-start(bf16[64,256]{1,0:T(8,128)(2,1)} %param.22) | copy-start | bytes 98308
  20.8 71.9 %copy-start.7 = (s32[4096]{0:T(1024)S(1)}, s32[4096]{0:T(1024)}, u32[]{:S(2)}) copy-start(s32[4096]{0:T(1024)} %param.18) | copy-start | bytes 49156
  23.1 72.2 %copy-start.8 = (s32[8]{0:T(128)S(1)}, s32[8]{0:T(128)}, u32[]{:S(2)}) copy-start(s32[8]{0:T(128)} %param.19) | copy-start | bytes 100
  24.3 102.3 %all-gather.7.cloned.1.call-start = ((), (), s32[]{:S(2)}) async-start(), calls=%async_computation.2 | async-start | bytes 2359296 | tf_op jit(solution)/shard_map/all_gather | solution.py:143
  25.3 161.2 %all-gather.9.cloned.1.call-start = ((), (), s32[]{:S(2)}) async-start(), calls=%async_computation.3 | async-start | bytes 2359296 | tf_op jit(solution)/shard_map/all_gather | solution.py:144
  26.0 205.2 %reduce-scatter.5.cloned.1.call-start = ((), (), s32[]{:S(2)}) async-start(), calls=%async_computation.5 | async-start | bytes 786432 | tf_op jit(solution)/shard_map/reduce_scatter | solution.py:222
  119.1 7.6 %copy-start.4 = (s32[2,4]{1,0:T(2,128)S(1)}, s32[2,4]{1,0:T(2,128)}, u32[]{:S(2)}) copy-start(s32[2,4]{1,0:T(2,128)} %lt.62) | copy-start | bytes 100
  126.4 122.4 %reduce-scatter.3.cloned.1.call-start = ((), (), s32[]{:S(2)}) async-start(), calls=%async_computation.4 | async-start | bytes 6291456 | tf_op jit(solution)/shard_map/reduce_scatter | solution.py:216
Sparse Core Ops, SparseCore 0:
  24.4 40.9 all-gather.10
  68.0 49.4 all-gather.6
  119.7 47.6 all-gather.8
  170.1 7.2 reduce-scatter.4
  231.3 17.4 reduce-scatter.2
where the time goes:
time: 258 us; the launch traced here: 255 us
  matrix products  84.5 us (33%)
  blocking collectives  58.2 us (23%)
  other arithmetic  48.6 us (19%)
  local copies, waits for them, and re-layouts  30.9 us (12%)
  waiting for transfers between devices  18.4 us (7%)
  between operations  14.1 us (5%)
    all_gather x2, blocking collectives, combined_all(): lax.all_gather(part.astype(kind), axis)  58.2 us
    dot_general x1, matrix products, attend_block(): jnp.einsum('tkgd,skd->kgts', queries, key_piece.reshape(count_rows, kv_lo...  31.4 us
    dot_general x1, matrix products, attend_block(): jnp.einsum('kgts,skd->kgtd', weights.astype(jnp.bfloat16), value_piece.re...  31.1 us
    reduce_sum x1, other arithmetic, attend_block(): totals = jnp.sum(weights, axis=-1)  28.4 us
    reduce_scatter x1, waiting for transfers between devices, on_device(): lax.psum_scatter(project_rows(prompt_attn, out_proj).astype(jnp.bfloat16)...  17.6 us
    dot_general x2, matrix products, project_rows(): return jnp.dot(rows_matrix, out_proj, preferred_element_type=jnp.float32)  15.3 us
    dynamic_slice x7, local copies, waits for them, and re-layouts, take(): part[k].astype(own.dtype)  6.48 us
  transfers between devices with their start and end apart: 5, of which 1 were waited for; matrix products, arithmetic and copies ran while one was open for 58% of the time, Pallas kernels for 0%

commit v1 on v0

v1 whole, which is shorter than its diff:
```python
import functools
import math

import jax
import jax.numpy as jnp
from jax import lax
from jax.experimental import pallas as pl
from jax.experimental.pallas import tpu as pltpu
from jax.sharding import PartitionSpec as P

HD = 128
WINDOW = 4096
PAGE = 128
MASKED = -1e30
FLOOR = -1e29
MESH = pl.DeviceIdType.MESH


def dot_t(a, b):
    return lax.dot_general(a, b, (((1,), (1,)), ((), ())), preferred_element_type=jnp.float32)


def wide(column, width):
    return jnp.concatenate([column] * (width // column.shape[1]), axis=1)


def kernel(
    n, back, q, k, v, lo, col_req, dq, dk, dv, ck, cv, w,
    out_p, out_d,
    kv, top, tot, acc, rows, ckv, cvv, wv, part, gathered, mine, att, outgoing, incoming,
    local_sem, zs, zr, ys, yr, ps, pr, fs, fr, ts, tr,
):
    me = lax.axis_index("seq")
    core = lax.axis_index("tp")
    other = 1 - core
    odd = lax.rem(me, 2)
    partner = me + 1 - 2 * odd
    tokens = q.shape[0]
    heads = q.shape[1] // HD
    groups = k.shape[1] // HD
    per = heads // groups
    reqs = dq.shape[0]
    scale = 1.0 / math.sqrt(HD)
    exp_scale = scale * math.log2(math.e)

    loads = [
        pltpu.make_async_copy(ck, ckv, local_sem.at[0]),
        pltpu.make_async_copy(cv, cvv, local_sem.at[1]),
        pltpu.make_async_copy(w, wv, local_sem.at[2]),
    ]
    for load in loads:
        load.start()

    barrier = pltpu.get_barrier_semaphore()

    def greet(d, carry):
        pl.semaphore_signal(
            barrier, inc=1, device_id={"seq": lax.rem(me + d, n)}, device_id_type=MESH
        )
        return carry

    lax.fori_loop(1, n, greet, 0)
    pl.semaphore_signal(barrier, inc=1, device_id={"tp": other}, device_id_type=MESH)
    pl.semaphore_wait(barrier, n)

    def source(s, g, i):
        if s == 0:
            return (k, v)[i].at[:, pl.ds(g * HD, HD)]
        return kv.at[s - 1, g, i]

    def along(s, g, i):
        return pltpu.make_async_remote_copy(
            src_ref=source(s, g, i),
            dst_ref=kv.at[s + 1, g, i],
            send_sem=zs.at[s // 2, g, i],
            recv_sem=zr.at[s // 2, g, i],
            device_id={"seq": lax.rem(me + 2, n)},
            device_id_type=MESH,
        )

    def across(s, h, g, i):
        return pltpu.make_async_remote_copy(
            src_ref=source(s, g, i),
            dst_ref=kv.at[2 * h - 2, g, i],
            send_sem=ys.at[h - 1, g, i],
            recv_sem=yr.at[h - 1, g, i],
            device_id={"seq": partner},
            device_id_type=MESH,
        )

    def forward(s, g, finish=False):
        act = (lambda c: c.wait_send()) if finish else (lambda c: c.start())
        if s + 2 <= back:
            @pl.when((me >= s) & (me + 2 < n))
            def _():
                for i in range(2):
                    act(along(s, g, i))

            @pl.when((me >= s) & (odd == 0))
            def _():
                for i in range(2):
                    act(across(s, s // 2 + 1, g, i))
        if s >= 2:
            @pl.when((me >= s) & (odd == 1))
            def _():
                for i in range(2):
                    act(across(s, s // 2, g, i))

    def arrive(s, g):
        @pl.when(me >= s)
        def _():
            for i in range(2):
                if s % 2 == 0:
                    along(s - 2, g, i).wait_recv()
                else:
                    across(s + 1, (s + 1) // 2, g, i).wait_recv()

        if s % 2 == 0:
            forward(s, g)

    def attend(s, g):
        def one_head(r, carry):
            head = g * per + r
            queries = q[:, pl.ds(pl.multiple_of(head * HD, HD), HD)]
            if s == 0:
                keys = k[:, g * HD:(g + 1) * HD]
                values = v[:, g * HD:(g + 1) * HD]
            else:
                keys = kv[s - 1, g, 0]
                values = kv[s - 1, g, 1]
            scores = dot_t(queries, keys)
            column = lax.broadcasted_iota(jnp.int32, (tokens, tokens), 1)
            limit = lo[head] - (me - s) * tokens
            allowed = column >= limit
            if s == 0:
                allowed = allowed & (
                    column <= lax.broadcasted_iota(jnp.int32, (tokens, tokens), 0)
                )
            scores = jnp.where(allowed, scores, MASKED)
            high = jnp.max(scores, axis=1, keepdims=True) * exp_scale
            high = jnp.broadcast_to(high, (tokens, HD))
            if s > 0:
                old = top[head]
                high = jnp.maximum(high, old)
            weights = jnp.exp2(scores * exp_scale - wide(high, tokens))
            total = jnp.broadcast_to(jnp.sum(weights, axis=1, keepdims=True), (tokens, HD))
            added = jnp.dot(
                weights.astype(jnp.bfloat16), values, preferred_element_type=jnp.float32
            )
            if s > 0:
                shrink = jnp.exp2(old - high)
                total = total + tot[head] * shrink
                added = added + acc[head] * shrink
            top[head] = high
            tot[head] = total
            acc[head] = added
            return carry

        @pl.when(me >= s)
        def _():
            lax.fori_loop(0, per, one_head, 0)

    def to_owner(head):
        return pltpu.make_async_remote_copy(
            src_ref=part.at[head],
            dst_ref=gathered.at[me],
            send_sem=ps.at[head],
            recv_sem=pr.at[me],
            device_id={"seq": head},
            device_id_type=MESH,
        )

    def decode_partials():
        loads[0].wait()
        loads[1].wait()
        pages = col_req.shape[0]
        step = math.gcd(pages, 8)
        row_req = lax.rem(
            lax.broadcasted_iota(jnp.int32, (per * reqs, step * PAGE), 0), reqs
        )
        for g in range(groups):
            queries = jnp.concatenate(
                [dq[:, (g * per + r) * HD:(g * per + r + 1) * HD] for r in range(per)], axis=0
            )

            def block(b, carry):
                high_old, total_old, acc_old = carry
                span = pl.ds(pl.multiple_of(b * step * PAGE, step * PAGE), step * PAGE)
                keys = ckv[span, g * HD:(g + 1) * HD]
                values = cvv[span, g * HD:(g + 1) * HD]
                reqs_of = col_req[pl.ds(pl.multiple_of(b * step, step), step), :]
                reqs_of = jnp.concatenate([reqs_of[i:i + 1, :] for i in range(step)], axis=1)
                scores = jnp.where(row_req == reqs_of, dot_t(queries, keys), MASKED)
                high = jnp.max(scores, axis=1, keepdims=True)
                high = jnp.maximum(high, FLOOR) * exp_scale
                high = jnp.maximum(jnp.broadcast_to(high, (per * reqs, HD)), high_old)
                weights = jnp.exp2(scores * exp_scale - wide(high, step * PAGE))
                total = jnp.sum(weights, axis=1, keepdims=True)
                shrink = jnp.exp2(high_old - high)
                added = jnp.dot(
                    weights.astype(jnp.bfloat16), values, preferred_element_type=jnp.float32
                )
                return (high, total + total_old * shrink, added + acc_old * shrink)

            zero = jnp.zeros((per * reqs, HD), jnp.float32)
            high, total, added = lax.fori_loop(
                0, pages // step, block, (zero + FLOOR * exp_scale, zero, zero)
            )
            for r in range(per):
                cut = slice(r * reqs, (r + 1) * reqs)
                part[g * per + r, 0] = high[cut]
                part[g * per + r, 1] = total[cut]
                part[g * per + r, 2] = added[cut]
        for head in range(heads):
            @pl.when(me != head)
            def _():
                to_owner(head).start()

    def from_owner(d):
        return pltpu.make_async_remote_copy(
            src_ref=mine,
            dst_ref=att.at[me],
            send_sem=fs.at[d - 1],
            recv_sem=fr.at[me],
            device_id={"seq": lax.rem(me + d, n)},
            device_id_type=MESH,
        )

    def wait_partial(j):
        return pltpu.make_async_remote_copy(
            src_ref=part.at[0],
            dst_ref=gathered.at[j],
            send_sem=ps.at[0],
            recv_sem=pr.at[j],
            device_id={"seq": partner},
            device_id_type=MESH,
        )

    def wait_final(head):
        return pltpu.make_async_remote_copy(
            src_ref=mine,
            dst_ref=att.at[head],
            send_sem=fs.at[0],
            recv_sem=fr.at[head],
            device_id={"seq": partner},
            device_id_type=MESH,
        )

    def decode_merge():
        @pl.when(me < heads)
        def _():
            head = me
            queries = dq[:, pl.ds(pl.multiple_of(head * HD, HD), HD)].astype(jnp.float32)
            group = pl.ds(pl.multiple_of((head // per) * HD, HD), HD)
            own = jnp.sum(queries * dk[:, group].astype(jnp.float32), axis=1, keepdims=True)
            own = jnp.broadcast_to(own * exp_scale, (reqs, HD))
            high = jnp.maximum(own, part[head, 0])
            shrink = jnp.exp2(part[head, 0] - high)
            weight = jnp.exp2(own - high)
            total = weight + part[head, 1] * shrink
            value = dv[:, group].astype(jnp.float32)
            summed = (
                weight.astype(jnp.bfloat16).astype(jnp.float32) * value
                + part[head, 2] * shrink
            )

            def take(d, carry):
                high_old, total_old, sum_old = carry
                j = lax.rem(me + d, n)
                wait_partial(j).wait_recv()
                fresh = jnp.maximum(high_old, gathered[j, 0])
                left = jnp.exp2(high_old - fresh)
                right = jnp.exp2(gathered[j, 0] - fresh)
                return (
                    fresh,
                    total_old * left + gathered[j, 1] * right,
                    sum_old * left + gathered[j, 2] * right,
                )

            high, total, summed = lax.fori_loop(1, n, take, (high, total, summed))
            final = (summed / total).astype(jnp.bfloat16)
            mine[...] = final

            def send(d, carry):
                from_owner(d).start()
                return carry

            lax.fori_loop(1, n, send, 0)

    for g in range(groups):
        forward(0, g)
    for g in range(groups):
        attend(0, g)
    arrive(2, 0)
    decode_partials()
    for g in range(1, groups):
        arrive(2, g)
    for g in range(groups):
        attend(2, g)
    for h in range(1, back // 2 + 1):
        for g in range(groups):
            if 2 * h + 2 <= back:
                arrive(2 * h + 2, g)
            arrive(2 * h - 1, g)
            attend(2 * h - 1, g)
        if h == 1:
            decode_merge()
        if 2 * h + 2 <= back:
            for g in range(groups):
                attend(2 * h + 2, g)

    half = tokens // 2
    half_reqs = reqs // 2
    for head in range(heads):
        cut = slice(head * HD, (head + 1) * HD)
        done = (acc[head] / tot[head]).astype(jnp.bfloat16)
        for c in range(2):
            rows[c, :half, cut] = done[c * half:(c + 1) * half]

        @pl.when(me == head)
        def _():
            for c in range(2):
                rows[c, half:, cut] = mine[c * half_reqs:(c + 1) * half_reqs]

        @pl.when(me != head)
        def _():
            wait_final(head).wait_recv()
            for c in range(2):
                rows[c, half:, cut] = att[head, c * half_reqs:(c + 1) * half_reqs]

    loads[2].wait()
    blocks = outgoing.shape[0]
    width = outgoing.shape[2]

    def exchange(b):
        return pltpu.make_async_remote_copy(
            src_ref=outgoing.at[b],
            dst_ref=incoming.at[b],
            send_sem=ts.at[b],
            recv_sem=tr.at[b],
            device_id={"tp": other},
            device_id_type=MESH,
        )

    def project(c, b):
        span = pl.ds(pl.multiple_of(b * width, width), width)
        return jnp.dot(rows[c], wv[:, span], preferred_element_type=jnp.float32)

    def give(b, carry):
        outgoing[b] = project(other, b).astype(jnp.bfloat16)
        exchange(b).start()
        return carry

    def keep(b, carry):
        own = project(core, b).astype(jnp.bfloat16).astype(jnp.float32)
        exchange(b).wait_recv()
        total = (own + incoming[b].astype(jnp.float32)).astype(jnp.bfloat16)
        span = pl.ds(pl.multiple_of(b * width, width), width)
        out_p[:, span] = total[:half]
        out_d[:, span] = total[half:]
        return carry

    lax.fori_loop(0, blocks, give, 0)
    lax.fori_loop(0, blocks, keep, 0)

    def sent(b, carry):
        exchange(b).wait_send()
        return carry

    lax.fori_loop(0, blocks, sent, 0)
    for s in range(0, back + 1, 2):
        for g in range(groups):
            forward(s, g, finish=True)
    for head in range(heads):
        @pl.when(me != head)
        def _():
            to_owner(head).wait_send()

    @pl.when(me < heads)
    def _():
        def sent_final(d, carry):
            from_owner(d).wait_send()
            return carry

        lax.fori_loop(1, n, sent_final, 0)


def on_device(
    n, prefill_query, prefill_key, prefill_value, doc_ids, head_window, dec_query, dec_key,
    dec_value, cache_key, cache_value, page_order, lengths, out_proj,
):
    tokens, width = prefill_query.shape
    heads = width // HD
    groups = prefill_key.shape[1] // HD
    reqs = dec_query.shape[0]
    model = out_proj.shape[1]
    pages = page_order.shape[0]
    reach = min(doc_ids.shape[0] // 2, WINDOW)
    back = -(-reach // tokens)
    back += back % 2

    my_start = lax.axis_index("seq") * tokens
    query_doc = lax.dynamic_slice_in_dim(doc_ids, my_start, tokens, 0)
    doc_start = jnp.sum((doc_ids[None, :] < query_doc[:, None]).astype(jnp.int32), axis=1)
    position = my_start + jnp.arange(tokens, dtype=jnp.int32)
    lo = jnp.maximum(doc_start[None, :], position[None, :] - head_window[:, None] + 1)[..., None]

    pages_request = pages * n // reqs
    owner = page_order // pages_request
    slot = page_order % pages_request
    member = owner[:, None] == jnp.arange(reqs, dtype=jnp.int32)[None, :]
    length = jnp.sum(jnp.where(member, lengths[None, :], 0), axis=1)
    place = slot[:, None] * PAGE + jnp.arange(PAGE, dtype=jnp.int32)[None, :]
    col_req = jnp.where(place < length[:, None], owner[:, None], -1)

    vmem = pl.BlockSpec(memory_space=pltpu.VMEM)
    hbm = pl.BlockSpec(memory_space=pl.ANY)
    block = 512
    blocks = model // block
    merged = (tokens + reqs) // 2
    dma = pltpu.SemaphoreType.DMA
    return pl.pallas_call(
        functools.partial(kernel, n, back),
        out_shape=(
            jax.ShapeDtypeStruct((tokens // 2, model), jnp.bfloat16),
            jax.ShapeDtypeStruct((reqs // 2, model), jnp.bfloat16),
        ),
        in_specs=[vmem] * 8 + [hbm] * 3,
        out_specs=(vmem, vmem),
        scratch_shapes=[
            pltpu.VMEM((back, groups, 2, tokens, HD), jnp.bfloat16),
            pltpu.VMEM((heads, tokens, HD), jnp.float32),
            pltpu.VMEM((heads, tokens, HD), jnp.float32),
            pltpu.VMEM((heads, tokens, HD), jnp.float32),
            pltpu.VMEM((2, merged, heads * HD), jnp.bfloat16),
            pltpu.VMEM(cache_key.shape, jnp.bfloat16),
            pltpu.VMEM(cache_value.shape, jnp.bfloat16),
            pltpu.VMEM(out_proj.shape, jnp.bfloat16),
            pltpu.VMEM((heads, 3, reqs, HD), jnp.float32),
            pltpu.VMEM((n, 3, reqs, HD), jnp.float32),
            pltpu.VMEM((reqs, HD), jnp.bfloat16),
            pltpu.VMEM((n, reqs, HD), jnp.bfloat16),
            pltpu.VMEM((blocks, merged, block), jnp.bfloat16),
            pltpu.VMEM((blocks, merged, block), jnp.bfloat16),
            dma((3,)),
            dma((back // 2, groups, 2)),
            dma((back // 2, groups, 2)),
            dma((back // 2, groups, 2)),
            dma((back // 2, groups, 2)),
            dma((heads,)),
            dma((n,)),
            dma((n - 1,)),
            dma((n,)),
            dma((blocks,)),
            dma((blocks,)),
        ],
        compiler_params=pltpu.CompilerParams(
            collective_id=0, has_side_effects=True, vmem_limit_bytes=60 * 1024 * 1024
        ),
    )(
        prefill_query, prefill_key, prefill_value, lo, col_req, dec_query, dec_key, dec_value,
        cache_key, cache_value, out_proj,
    )


def solution(mesh):
    placed = (
        P(("rep", "seq"), "tp"),
        P(("rep", "seq"), "tp"),
        P(("rep", "seq"), "tp"),
        P("rep"),
        P("tp"),
        P("rep", "tp"),
        P("rep", "tp"),
        P("rep", "tp"),
        P(("rep", "seq"), "tp"),
        P(("rep", "seq"), "tp"),
        P(("rep", "seq")),
        P("rep"),
        P("tp", None),
    )
    return jax.shard_map(
        functools.partial(on_device, mesh.shape["seq"]),
        mesh=mesh,
        in_specs=placed,
        out_specs=(P(("rep", "seq", "tp"), None), P(("rep", "tp"), None)),
        check_vma=False,
    )
```

time: 258 us -> 89.3 us (0.35)
  matrix products: 84.5 us -> 0 us
  Pallas kernels: 0 us -> 77.5 us
  blocking collectives: 58.2 us -> 0 us
  other arithmetic: 48.6 us -> 6.23 us
  local copies, waits for them, and re-layouts: 30.9 us -> 4.64 us
  waiting for transfers between devices: 18.4 us -> 0 us
  between operations: 14.1 us -> 0.66 us
    dot_general x9 -> x0, matrix products: 84.5 us -> none  [the longest x1 31.4 us: attend_block(): jnp.einsum('tkgd,skd->kgts', queries, key_piece.reshape(count_rows, kv_lo...]
    pallas_call x0 -> x1, Pallas kernels: none -> 77.5 us  [on_device(): pl.pallas_call(functools.partial(kernel, n, back), out_shape=(jax.ShapeDt...]
    all_gather x2 -> x0, blocking collectives: 58.2 us -> none  [combined_all(): lax.all_gather(part.astype(kind), axis)]
    reduce_sum x2, other arithmetic: 28.6 us -> 2.51 us  [the longest x1 1.68 us: on_device(): jnp.sum((doc_ids[None, :] < query_doc[:, None]).astype(jnp.int32), axis=1)]
    reduce_scatter x2 -> x0, waiting for transfers between devices: 17.6 us -> none  [the longest x1 17.6 us: on_device(): lax.psum_scatter(project_rows(prompt_attn, out_proj).astype(jnp.bfloat16)...]
    add x15 -> x1, other arithmetic: 8.98 us -> 0.01 us  [on_device(): position = my_start + jnp.arange(tokens, dtype=jnp.int32)]
    reshape x7 -> x0, local copies, waits for them, and re-layouts: 8.06 us -> none  [the longest x1 4.03 us: on_device(): page_keys = cache_key.reshape(page_count, PAGE, kv_local, HD)]
    dynamic_slice x8 -> x1, local copies, waits for them, and re-layouts: 6.55 us -> 0.77 us  [on_device(): query_doc = lax.dynamic_slice_in_dim(doc_ids, my_start, tokens, 0)]
  transfers between devices with their start and end apart: 5 -> 0, of which waited for: 1 -> 0; matrix products, arithmetic and copies ran while one was open for 58% -> 0% of each run, Pallas kernels for 0% -> 0%
where the time goes in v1:
time: 89.3 us; the launch traced here: 89 us
  Pallas kernels  77.5 us (87%)
  other arithmetic  6.23 us (7%)
  local copies, waits for them, and re-layouts  4.64 us (5%)
    pallas_call x1, Pallas kernels, on_device(): pl.pallas_call(functools.partial(kernel, n, back), out_shape=(jax.ShapeDt...  77.5 us
    unnamed x4, local copies, waits for them, and re-layouts  3.88 us
    max x1, other arithmetic, on_device(): jnp.maximum(doc_start[None, :], position[None, :] - head_window[:, None]...  2.36 us

profile of v1, /device:TPU:18, one launch (start us, length us, event | category | flops | bytes accessed | tf_op | source)
XLA Modules:
  0.0 89.0 jit_solution(717817137733777377)
XLA Ops:
  0.6 0.7 fusion.1
  1.3 0.8 select_reduce_fusion
  2.1 0.8 dynamic_slice.3
  2.9 1.7 %convert_reduce_fusion = s32[512]{0:T(512)S(1)} fusion(s32[4096]{0:T(1024)} %param.16, s32[512]{0:T(512)S(1)} %dynamic_slice.3), kind=kLoop, calls=%fused_computation | loop fusion | flops 6290944 | bytes 20480 | tf_op jit(solution)/shard_map/reduce_sum | solution.py:404
  4.6 0.7 fusion.col_req
  5.3 2.4 %add_maximum_fusion.lo = s32[8,512,1]{2,1,0:T(8,128)} fusion(s32[512]{0:T(512)S(1)} %convert_reduce_fusion, s32[8]{0:T(128)} %param.17, s32[512]{0:T(512)S(1)} %iota_add_fusion), kind=kLoop, calls=%fused_computation.1 | loop fusion | flops 12288 | bytes 20512 | tf_op jit(solution)/shard_map/max | solution.py:406
  7.6 77.5 %shard_map.140 = (bf16[256,4096]{1,0:T(8,128)(2,1)}, bf16[32,4096]{1,0:T(8,128)(2,1)}) custom-call(bf16[512,1024]{1,0:T(8,128)(2,1)} %q.1, bf16[512,256]{1,0:T(8,128)(2,1)} %k.1, bf16[512,256]{1,0:T(8,128)(2,1)} %v.1, s32[8,512,1]{2,1,0:T(8,128)} %add_maximum_fusion.lo, s32[32,128]{1,0:T(8,128)} %fusion.col_req, bf16[64,1024]{1,0:T(8,128)(2,1)} %dq.1, ...), custom_call_target="tpu_custom_call" | custom-call | tf_op jit(solution)/shard_map/pallas_call | solution.py:422
  85.1 0.0 copy-start
  85.1 3.2 %copy.18 = bf16[256,4096]{1,0:T(8,128)(2,1)} copy(bf16[256,4096]{1,0:T(8,128)(2,1)} %get-tuple-element.6) | data formatting | bytes 4194304
  88.3 0.0 copy-done
  88.3 0.7 copy.19
  (1 shorter events, 0.0 us)
Async XLA Ops:
  85.1 3.2 %copy-start = (bf16[32,4096]{1,0:T(8,128)(2,1)S(1)}, bf16[32,4096]{1,0:T(8,128)(2,1)}, u32[]{:S(2)}) copy-start(bf16[32,4096]{1,0:T(8,128)(2,1)} %get-tuple-element.7) | copy-start | bytes 786436

commit v2 on v1

--- a/solution.py
+++ b/solution.py
@@ -11,6 +11,7 @@
 HD = 128
 WINDOW = 4096
 PAGE = 128
+DOCS = 4
 MASKED = -1e30
 FLOOR = -1e29
 MESH = pl.DeviceIdType.MESH
@@ -25,9 +26,10 @@
 
 
 def kernel(
-    n, back, q, k, v, lo, col_req, dq, dk, dv, ck, cv, w,
+    n, back, pages_request, q, k, v, docs, windows, order, lengths, dq, dk, dv, ck, cv, w,
     out_p, out_d,
-    kv, top, tot, acc, rows, ckv, cvv, wv, part, gathered, mine, att, outgoing, incoming,
+    kv, top, tot, acc, lo, rows, ckv, cvv, wv, part, part_log, gathered, gathered_log, mine, att,
+    outgoing, incoming,
     local_sem, zs, zr, ys, yr, ps, pr, fs, fr, ts, tr,
 ):
     me = lax.axis_index("seq")
@@ -63,6 +65,15 @@
     pl.semaphore_signal(barrier, inc=1, device_id={"tp": other}, device_id_type=MESH)
     pl.semaphore_wait(barrier, n)
 
+    position = me * tokens + lax.broadcasted_iota(jnp.int32, (tokens, HD), 0)
+    place = position.astype(jnp.float32)
+    start = jnp.zeros((tokens, HD), jnp.float32)
+    for document in range(1, DOCS):
+        before = (docs[...] < document).astype(jnp.float32)
+        before = jnp.sum(jnp.sum(before, axis=0, keepdims=True), axis=1, keepdims=True)
+        start = jnp.where(before <= place, jnp.maximum(start, before), start)
+    lo[...] = start.astype(jnp.int32)
+
     def source(s, g, i):
         if s == 0:
             return (k, v)[i].at[:, pl.ds(g * HD, HD)]
@@ -130,8 +141,9 @@
                 values = kv[s - 1, g, 1]
             scores = dot_t(queries, keys)
             column = lax.broadcasted_iota(jnp.int32, (tokens, tokens), 1)
-            limit = lo[head] - (me - s) * tokens
-            allowed = column >= limit
+            place = me * tokens + lax.broadcasted_iota(jnp.int32, (tokens, HD), 0)
+            limit = jnp.maximum(lo[...], place - windows[head] + 1) - (me - s) * tokens
+            allowed = column >= wide(limit, tokens)
             if s == 0:
                 allowed = allowed & (
                     column <= lax.broadcasted_iota(jnp.int32, (tokens, tokens), 0)
@@ -161,22 +173,25 @@
             lax.fori_loop(0, per, one_head, 0)
 
     def to_owner(head):
-        return pltpu.make_async_remote_copy(
-            src_ref=part.at[head],
-            dst_ref=gathered.at[me],
-            send_sem=ps.at[head],
-            recv_sem=pr.at[me],
-            device_id={"seq": head},
-            device_id_type=MESH,
-        )
+        return [
+            pltpu.make_async_remote_copy(
+                src_ref=src.at[head],
+                dst_ref=dst.at[me],
+                send_sem=ps.at[head, i],
+                recv_sem=pr.at[me, i],
+                device_id={"seq": head},
+                device_id_type=MESH,
+            )
+            for i, (src, dst) in enumerate(((part, gathered), (part_log, gathered_log)))
+        ]
 
     def decode_partials():
         loads[0].wait()
         loads[1].wait()
-        pages = col_req.shape[0]
+        pages = order.shape[0]
         step = math.gcd(pages, 8)
-        row_req = lax.rem(
-            lax.broadcasted_iota(jnp.int32, (per * reqs, step * PAGE), 0), reqs
+        row_req = jnp.concatenate(
+            [lax.broadcasted_iota(jnp.int32, (reqs, step * PAGE), 0)] * per, axis=0
         )
         for g in range(groups):
             queries = jnp.concatenate(
@@ -188,8 +203,14 @@
                 span = pl.ds(pl.multiple_of(b * step * PAGE, step * PAGE), step * PAGE)
                 keys = ckv[span, g * HD:(g + 1) * HD]
                 values = cvv[span, g * HD:(g + 1) * HD]
-                reqs_of = col_req[pl.ds(pl.multiple_of(b * step, step), step), :]
-                reqs_of = jnp.concatenate([reqs_of[i:i + 1, :] for i in range(step)], axis=1)
+                lane = lax.broadcasted_iota(jnp.int32, (1, PAGE), 1)
+                reqs_of = []
+                for i in range(step):
+                    page = order[b * step + i]
+                    owner = page // pages_request
+                    left = lengths[owner] - (page - owner * pages_request) * PAGE
+                    reqs_of.append(jnp.where(lane < left, owner, -1))
+                reqs_of = jnp.concatenate(reqs_of, axis=1)
                 scores = jnp.where(row_req == reqs_of, dot_t(queries, keys), MASKED)
                 high = jnp.max(scores, axis=1, keepdims=True)
                 high = jnp.maximum(high, FLOOR) * exp_scale
@@ -208,13 +229,20 @@
             )
             for r in range(per):
                 cut = slice(r * reqs, (r + 1) * reqs)
-                part[g * per + r, 0] = high[cut]
-                part[g * per + r, 1] = total[cut]
-                part[g * per + r, 2] = added[cut]
+                some = total[cut] > 0.0
+                whole = jnp.where(some, total[cut], 1.0)
+                part[g * per + r] = (added[cut] / whole).astype(jnp.bfloat16)
+                level = jnp.where(some, high[cut] + jnp.log2(whole), FLOOR)
+                if reqs < HD:
+                    level = jnp.concatenate(
+                        [level, jnp.zeros((HD - reqs, HD), jnp.float32)], axis=0
+                    )
+                part_log[g * per + r] = level.T[:8]
         for head in range(heads):
             @pl.when(me != head)
             def _():
-                to_owner(head).start()
+                for copy in to_owner(head):
+                    copy.start()
 
     def from_owner(d):
         return pltpu.make_async_remote_copy(
@@ -227,14 +255,15 @@
         )
 
     def wait_partial(j):
-        return pltpu.make_async_remote_copy(
-            src_ref=part.at[0],
-            dst_ref=gathered.at[j],
-            send_sem=ps.at[0],
-            recv_sem=pr.at[j],
-            device_id={"seq": partner},
-            device_id_type=MESH,
-        )
+        for i, (src, dst) in enumerate(((part, gathered), (part_log, gathered_log))):
+            pltpu.make_async_remote_copy(
+                src_ref=src.at[0],
+                dst_ref=dst.at[j],
+                send_sem=ps.at[0, i],
+                recv_sem=pr.at[j, i],
+                device_id={"seq": partner},
+                device_id_type=MESH,
+            ).wait_recv()
 
     def wait_final(head):
         return pltpu.make_async_remote_copy(
@@ -254,30 +283,27 @@
             group = pl.ds(pl.multiple_of((head // per) * HD, HD), HD)
             own = jnp.sum(queries * dk[:, group].astype(jnp.float32), axis=1, keepdims=True)
             own = jnp.broadcast_to(own * exp_scale, (reqs, HD))
-            high = jnp.maximum(own, part[head, 0])
-            shrink = jnp.exp2(part[head, 0] - high)
-            weight = jnp.exp2(own - high)
-            total = weight + part[head, 1] * shrink
             value = dv[:, group].astype(jnp.float32)
-            summed = (
-                weight.astype(jnp.bfloat16).astype(jnp.float32) * value
-                + part[head, 2] * shrink
-            )
-
-            def take(d, carry):
+
+            def join(carry, logs, parts):
                 high_old, total_old, sum_old = carry
-                j = lax.rem(me + d, n)
-                wait_partial(j).wait_recv()
-                fresh = jnp.maximum(high_old, gathered[j, 0])
+                level = jnp.broadcast_to(logs[:1], (HD, HD)).T[:reqs]
+                fresh = jnp.maximum(high_old, level)
                 left = jnp.exp2(high_old - fresh)
-                right = jnp.exp2(gathered[j, 0] - fresh)
+                right = jnp.exp2(level - fresh)
                 return (
                     fresh,
-                    total_old * left + gathered[j, 1] * right,
-                    sum_old * left + gathered[j, 2] * right,
+                    total_old * left + right,
+                    sum_old * left + parts.astype(jnp.float32) * right,
                 )
 
-            high, total, summed = lax.fori_loop(1, n, take, (high, total, summed))
+            def take(d, carry):
+                j = lax.rem(me + d, n)
+                wait_partial(j)
+                return join(carry, gathered_log[j], gathered[j])
+
+            carry = join((own, jnp.ones_like(own), value), part_log[head], part[head])
+            high, total, summed = lax.fori_loop(1, n, take, carry)
             final = (summed / total).astype(jnp.bfloat16)
             mine[...] = final
 
@@ -374,7 +400,8 @@
     for head in range(heads):
         @pl.when(me != head)
         def _():
-            to_owner(head).wait_send()
+            for copy in to_owner(head):
+                copy.wait_send()
 
     @pl.when(me < heads)
     def _():
@@ -399,45 +426,37 @@
     back = -(-reach // tokens)
     back += back % 2
 
-    my_start = lax.axis_index("seq") * tokens
-    query_doc = lax.dynamic_slice_in_dim(doc_ids, my_start, tokens, 0)
-    doc_start = jnp.sum((doc_ids[None, :] < query_doc[:, None]).astype(jnp.int32), axis=1)
-    position = my_start + jnp.arange(tokens, dtype=jnp.int32)
-    lo = jnp.maximum(doc_start[None, :], position[None, :] - head_window[:, None] + 1)[..., None]
-
-    pages_request = pages * n // reqs
-    owner = page_order // pages_request
-    slot = page_order % pages_request
-    member = owner[:, None] == jnp.arange(reqs, dtype=jnp.int32)[None, :]
-    length = jnp.sum(jnp.where(member, lengths[None, :], 0), axis=1)
-    place = slot[:, None] * PAGE + jnp.arange(PAGE, dtype=jnp.int32)[None, :]
-    col_req = jnp.where(place < length[:, None], owner[:, None], -1)
-
+    pages_request = page_order.shape[0] * n // reqs
+    docs = doc_ids.reshape(-1, HD)
     vmem = pl.BlockSpec(memory_space=pltpu.VMEM)
     hbm = pl.BlockSpec(memory_space=pl.ANY)
+    smem = pl.BlockSpec(memory_space=pltpu.SMEM)
     block = 512
     blocks = model // block
     merged = (tokens + reqs) // 2
     dma = pltpu.SemaphoreType.DMA
     return pl.pallas_call(
-        functools.partial(kernel, n, back),
+        functools.partial(kernel, n, back, pages_request),
         out_shape=(
             jax.ShapeDtypeStruct((tokens // 2, model), jnp.bfloat16),
             jax.ShapeDtypeStruct((reqs // 2, model), jnp.bfloat16),
         ),
-        in_specs=[vmem] * 8 + [hbm] * 3,
+        in_specs=[vmem] * 4 + [smem] * 3 + [vmem] * 3 + [hbm] * 3,
         out_specs=(vmem, vmem),
         scratch_shapes=[
             pltpu.VMEM((back, groups, 2, tokens, HD), jnp.bfloat16),
             pltpu.VMEM((heads, tokens, HD), jnp.float32),
             pltpu.VMEM((heads, tokens, HD), jnp.float32),
             pltpu.VMEM((heads, tokens, HD), jnp.float32),
+            pltpu.VMEM((tokens, HD), jnp.int32),
             pltpu.VMEM((2, merged, heads * HD), jnp.bfloat16),
             pltpu.VMEM(cache_key.shape, jnp.bfloat16),
             pltpu.VMEM(cache_value.shape, jnp.bfloat16),
             pltpu.VMEM(out_proj.shape, jnp.bfloat16),
-            pltpu.VMEM((heads, 3, reqs, HD), jnp.float32),
-            pltpu.VMEM((n, 3, reqs, HD), jnp.float32),
+            pltpu.VMEM((heads, reqs, HD), jnp.bfloat16),
+            pltpu.VMEM((heads, 8, HD), jnp.float32),
+            pltpu.VMEM((n, reqs, HD), jnp.bfloat16),
+            pltpu.VMEM((n, 8, HD), jnp.float32),
             pltpu.VMEM((reqs, HD), jnp.bfloat16),
             pltpu.VMEM((n, reqs, HD), jnp.bfloat16),
             pltpu.VMEM((blocks, merged, block), jnp.bfloat16),
@@ -447,8 +466,8 @@
             dma((back // 2, groups, 2)),
             dma((back // 2, groups, 2)),
             dma((back // 2, groups, 2)),
-            dma((heads,)),
-            dma((n,)),
+            dma((heads, 2)),
+            dma((n, 2)),
             dma((n - 1,)),
             dma((n,)),
             dma((blocks,)),
@@ -458,8 +477,8 @@
             collective_id=0, has_side_effects=True, vmem_limit_bytes=60 * 1024 * 1024
         ),
     )(
-        prefill_query, prefill_key, prefill_value, lo, col_req, dec_query, dec_key, dec_value,
-        cache_key, cache_value, out_proj,
+        prefill_query, prefill_key, prefill_value, docs, head_window, page_order, lengths,
+        dec_query, dec_key, dec_value, cache_key, cache_value, out_proj,
     )
 
 

time: 89.3 us -> 67.3 us (0.75)
  Pallas kernels: 77.5 us -> 62.6 us
  other arithmetic: 6.23 us -> 0 us
    pallas_call x1, Pallas kernels: 77.5 us -> 62.6 us  [on_device(): pl.pallas_call(functools.partial(kernel, n, back, pages_request), out_sha...]
    reduce_sum x2 -> x0, other arithmetic: 2.51 us -> none  [the longest x1 1.68 us: on_device(): jnp.sum((doc_ids[None, :] < query_doc[:, None]).astype(jnp.int32), axis=1)]
    max x1 -> x0, other arithmetic: 2.36 us -> none  [on_device(): jnp.maximum(doc_start[None, :], position[None, :] - head_window[:, None]...]
where the time goes in v2:
time: 67.3 us; the launch traced here: 67.1 us
  Pallas kernels  62.6 us (93%)
  local copies, waits for them, and re-layouts  3.88 us (6%)
    pallas_call x1, Pallas kernels, on_device(): pl.pallas_call(functools.partial(kernel, n, back, pages_request), out_sha...  62.6 us
    unnamed x4, local copies, waits for them, and re-layouts  3.88 us

profile of v2, /device:TPU:18, one launch (start us, length us, event | category | flops | bytes accessed | tf_op | source)
XLA Modules:
  0.0 67.1 jit_solution(15179731778892471648)
XLA Ops:
  0.6 62.6 %shard_map.140 = (bf16[256,4096]{1,0:T(8,128)(2,1)}, bf16[32,4096]{1,0:T(8,128)(2,1)}) custom-call(bf16[512,1024]{1,0:T(8,128)(2,1)} %q.1, bf16[512,256]{1,0:T(8,128)(2,1)} %k.1, bf16[512,256]{1,0:T(8,128)(2,1)} %v.1, s32[32,128]{1,0:T(8,128)} %bitcast.1, s32[8]{0:T(128)} %windows.1, s32[32]{0:T(128)} %order.1, s32[64]{0:T(128)} %lengths.1, ...), custom_call_target="tpu_custom_call" | custom-call | tf_op jit(solution)/shard_map/pallas_call | solution.py:438
  63.2 0.0 copy-start
  63.2 3.2 %copy.17 = bf16[256,4096]{1,0:T(8,128)(2,1)} copy(bf16[256,4096]{1,0:T(8,128)(2,1)} %get-tuple-element.4) | data formatting | bytes 4194304
  66.4 0.0 copy-done
  66.4 0.7 %copy.18 = bf16[32,4096]{1,0:T(8,128)(2,1)} copy(bf16[32,4096]{1,0:T(8,128)(2,1)S(1)} %copy-done) | data formatting | bytes 524288
Async XLA Ops:
  63.2 3.2 %copy-start = (bf16[32,4096]{1,0:T(8,128)(2,1)S(1)}, bf16[32,4096]{1,0:T(8,128)(2,1)}, u32[]{:S(2)}) copy-start(bf16[32,4096]{1,0:T(8,128)(2,1)} %get-tuple-element.5) | copy-start | bytes 786436
